TPU v7x, 32 devices: a whole 2x2x4 slice. The times are simulated.
32 devices in a mesh: row: 4 (over y, x), col: 8 (over z, core).
Axes of the slice: x: 2, y: 2, z: 4, core: 2. Of those that a mesh axis runs over, the one named last changes fastest.
Arguments:
- amplitudes: bfloat16 [800, 800, 768], P('row', 'col'), may hold values from -6 to 6
- integrals: bfloat16 [800, 800, 256], P('row', 'col'), may hold values from -0.375 to 0.375
- window_index: int32 [256], replicated, may hold values from 0 to 639999, as said below
Outputs:
- residual: bfloat16 [800, 800, 768], P('row', 'col')
- pair_energy: float32 [768], replicated
Inputs may be any that keep to these rules, and one draw needn't show every extreme that they name: `window_index`: the window pairs are distinct; pair k lies in the block of a rows and b columns owned by device number k // 8 in row-major order of the (a, b) device grid, 8 pairs for each block.
All inputs are finite; a program needn't handle non-finite values.
Results may differ from a plain program's by a relative error of at most 0.001.
Values may be sent and summed in bfloat16 or wider, within the bound.
A program may use at most 256 MiB of HBM per device.

v0:
```python
import functools

import jax
import jax.numpy as jnp
from jax import lax
from jax.experimental import pallas as pl
from jax.experimental.pallas import tpu as pltpu
from jax.sharding import PartitionSpec as P

MESH = pl.DeviceIdType.MESH


def exchange_kernel(nrows, ncols, own_ref, out_ref, send_sems, recv_sems):
    count = nrows * ncols
    me = lax.axis_index("row") * ncols + lax.axis_index("col")

    def place(step):
        other = lax.rem(me + step, count)
        return (other // ncols, lax.rem(other, ncols))

    barrier = pltpu.get_barrier_semaphore()

    def greet(step, carry):
        pl.semaphore_signal(barrier, inc=1, device_id=place(step), device_id_type=MESH)
        return carry

    lax.fori_loop(1, count, greet, 0)
    pl.semaphore_wait(barrier, count - 1)

    def copy(step, slot):
        return pltpu.make_async_remote_copy(
            src_ref=own_ref,
            dst_ref=out_ref.at[slot],
            send_sem=send_sems.at[step],
            recv_sem=recv_sems.at[step],
            device_id=place(step),
            device_id_type=MESH,
        )

    def send(step, carry):
        copy(step, me).start()
        return carry

    lax.fori_loop(1, count, send, 0)
    out_ref[me] = own_ref[...]

    def finish(step, carry):
        source = lax.rem(me + count - step, count)
        copy(step, source).wait_recv()
        copy(step, me).wait_send()
        return carry

    lax.fori_loop(1, count, finish, 0)


def exchange(block, nrows, ncols, collective_id):
    count = nrows * ncols
    return pl.pallas_call(
        functools.partial(exchange_kernel, nrows, ncols),
        out_shape=jax.ShapeDtypeStruct((count,) + block.shape, block.dtype),
        in_specs=[pl.BlockSpec(memory_space=pltpu.VMEM)],
        out_specs=pl.BlockSpec(memory_space=pltpu.VMEM),
        scratch_shapes=[
            pltpu.SemaphoreType.DMA((count,)),
            pltpu.SemaphoreType.DMA((count,)),
        ],
        compiler_params=pltpu.CompilerParams(collective_id=collective_id, has_side_effects=True),
    )(block)


ROWS = 2000
SUB = 200


def largest_divisor(extent, most, multiple):
    fits = [d for d in range(multiple, min(extent, most) + 1, multiple) if extent % d == 0]
    return max(fits) if fits else extent


def ladder_kernel(sub, chunk, amps_ref, ints_ref, cols_ref, residual_ref, energy_ref, total_ref):
    rows, pairs = amps_ref.shape

    @pl.when(pl.program_id(0) == 0)
    def _():
        total_ref[...] = jnp.zeros_like(total_ref)

    for start in range(0, pairs, chunk):
        span = slice(start, start + chunk)
        total = jnp.zeros((8, chunk), jnp.float32)
        for low in range(0, rows, sub):
            part = slice(low, low + sub)
            full = jnp.dot(ints_ref[part], cols_ref[:, span], preferred_element_type=jnp.float32)
            residual_ref[part, span] = full.astype(residual_ref.dtype)
            weighted = amps_ref[part, span].astype(jnp.float32) * full
            total = total + jnp.sum(weighted.reshape(sub // 8, 8, chunk), axis=0)
        total_ref[:, span] += total

    @pl.when(pl.program_id(0) == pl.num_programs(0) - 1)
    def _():
        energy_ref[...] = jnp.sum(total_ref[...], axis=0, keepdims=True)


def ladder(amplitudes, integrals, columns):
    cells, pairs = amplitudes.shape
    window = integrals.shape[1]
    rows = largest_divisor(cells, ROWS, 8)
    sub = largest_divisor(rows, SUB, 8)
    chunk = 256 if pairs % 256 == 0 else pairs
    return pl.pallas_call(
        functools.partial(ladder_kernel, sub, chunk),
        grid=(cells // rows,),
        out_shape=(
            jax.ShapeDtypeStruct((cells, pairs), jnp.bfloat16),
            jax.ShapeDtypeStruct((1, pairs), jnp.float32),
        ),
        in_specs=[
            pl.BlockSpec((rows, pairs), lambda i: (i, 0)),
            pl.BlockSpec((rows, window), lambda i: (i, 0)),
            pl.BlockSpec((window, pairs), lambda i: (0, 0)),
        ],
        out_specs=(
            pl.BlockSpec((rows, pairs), lambda i: (i, 0)),
            pl.BlockSpec((1, pairs), lambda i: (0, 0)),
        ),
        scratch_shapes=[pltpu.VMEM((8, pairs), jnp.float32)],
        compiler_params=pltpu.CompilerParams(
            dimension_semantics=("arbitrary",), vmem_limit_bytes=60 * 1024 * 1024
        ),
    )(amplitudes, integrals, columns)


def shards(amplitudes, integrals, window_index):
    block_rows, block_cols, pairs = amplitudes.shape
    window = integrals.shape[2]
    ncols = lax.axis_size("col")
    nrows = lax.axis_size("row")
    per_device = window // (nrows * ncols)
    row_rank = lax.axis_index("row")
    col_rank = lax.axis_index("col")
    linear_rank = row_rank * ncols + col_rank
    owned_index = lax.dynamic_slice_in_dim(window_index, linear_rank * per_device, per_device)
    virtuals = block_rows * nrows
    row_offset = owned_index // virtuals - row_rank * block_rows
    col_offset = owned_index % virtuals - col_rank * block_cols
    owned = amplitudes[row_offset, col_offset]
    columns = exchange(owned, nrows, ncols, 0).reshape(window, pairs)
    cells = block_rows * block_cols
    residual, partial_value = ladder(
        amplitudes.transpose(1, 0, 2).reshape(cells, pairs),
        integrals.transpose(1, 0, 2).reshape(cells, window),
        columns,
    )
    residual = residual.reshape(block_cols, block_rows, pairs).transpose(1, 0, 2)
    values = exchange(partial_value, nrows, ncols, 1)
    pair_energy = jnp.sum(values[:, 0, :], axis=0) / virtuals
    return (residual, pair_energy)


def solution(mesh):
    return jax.shard_map(
        shards,
        mesh=mesh,
        in_specs=(P("row", "col", None), P("row", "col", None), P()),
        out_specs=(P("row", "col", None), P()),
        check_vma=False,
    )
```

profile of v0, /device:TPU:0, one launch (start us, length us, event | category | flops | bytes accessed | tf_op | source)
XLA Modules:
  0.0 61.1 jit_solution(17818447023833055575)
XLA Ops:
  0.6 0.8 %fusion.3 = s32[8]{0:T(128)S(1)} fusion(s32[256]{0:T(256)} %param.5, s32[]{:T(128)S(6)} %select_n.21, s32[]{:T(128)S(6)} %mul.15, s32[]{:T(128)S(6)} %mul.14), kind=kLoop, calls=%fused_computation.9 | loop fusion | flops 200 | bytes 76 | tf_op jit(solution)/shard_map/concatenate | solution.py:145
  1.4 2.0 %gather_fusion = bf16[8,768]{1,0:T(8,128)(2,1)} fusion(bf16[200,100,768]{2,0,1:T(8,128)(2,1)} %param.3, s32[8]{0:T(128)S(1)} %fusion.3), kind=kCustom, calls=%fused_computation | custom fusion | bytes 24640 | tf_op jit(solution)/shard_map/gather | solution.py:145
  3.4 18.2 %shard_map.50 = bf16[32,8,768]{2,1,0:T(8,128)(2,1)} custom-call(bf16[8,768]{1,0:T(8,128)(2,1)} %gather_fusion), custom_call_target="tpu_custom_call" | custom-call | tf_op jit(solution)/shard_map/pallas_call | solution.py:58
  21.6 27.8 %shard_map.51 = (bf16[20000,768]{1,0:T(8,128)(2,1)}, f32[1,768]{1,0:T(1,128)}) custom-call(bf16[20000,768]{1,0:T(8,128)(2,1)} %bitcast.10, bf16[20000,256]{1,0:T(8,128)(2,1)} %bitcast.11, bf16[256,768]{1,0:T(8,128)(2,1)} %bitcast.12), custom_call_target="tpu_custom_call" | custom-call | tf_op jit(solution)/shard_map/pallas_call | solution.py:109
  49.3 10.2 %shard_map.52 = f32[32,1,768]{2,1,0:T(1,128)} custom-call(f32[1,768]{1,0:T(1,128)} %get-tuple-element.5.own_ref), custom_call_target="tpu_custom_call" | custom-call | tf_op jit(solution)/shard_map/pallas_call | solution.py:58
  59.5 1.0 %reduce_sum.9 = f32[768]{0:T(1024)S(1)} reduce(f32[32,1,768]{2,1,0:T(1,128)} %shard_map.52, f32[]{:T(128)} %constant.43.clone.1), dimensions={0,1}, to_apply=%region_0.1 | reduce | flops 23808 | bytes 101380 | tf_op jit(solution)/shard_map/reduce_sum | solution.py:155
  60.5 0.6 broadcast_multiply_fusion
where the time goes:
time: 61.4 us; the launch traced here: 61.1 us
  Pallas kernels  56.1 us (91%)
  other arithmetic  2.34 us (4%)
  local copies, waits for them, and re-layouts  1.97 us (3%)
  between operations  0.65 us (1%)
    pallas_call x2, Pallas kernels, exchange(): pl.pallas_call(functools.partial(exchange_kernel, nrows, ncols), out_shap...  28.4 us
    pallas_call x1, Pallas kernels, ladder(): pl.pallas_call(functools.partial(ladder_kernel, sub, chunk), grid=(cells...  27.8 us
    gather x1, local copies, waits for them, and re-layouts, shards(): owned = amplitudes[row_offset, col_offset]  1.97 us

commit v1 on v0

v1 whole, which is shorter than its diff:
```python
import functools

import jax
import jax.numpy as jnp
from jax import lax
from jax.experimental import pallas as pl
from jax.experimental.pallas import tpu as pltpu
from jax.sharding import PartitionSpec as P

MESH = pl.DeviceIdType.MESH
ROWS = 2000
OUT_ROWS = 1000
MIB = 1024 * 1024


def largest_divisor(extent, most, multiple):
    fits = [d for d in range(multiple, min(extent, most) + 1, multiple) if extent % d == 0]
    return max(fits) if fits else extent


def gather_kernel(
    nrows, ncols, rows, own_ref, ints_ref, amps_ref, out_ref, energy_ref,
    held, product, partial, values, load_sems, send_sems, recv_sems, esend_sems, erecv_sems,
):
    count = nrows * ncols
    cells = ints_ref.shape[0]
    chunks = cells // rows
    me = lax.axis_index("row") * ncols + lax.axis_index("col")

    def place(step):
        other = lax.rem(me + step, count)
        return (other // ncols, lax.rem(other, ncols))

    def load(i):
        span = pl.ds(i * rows, rows)
        return pltpu.make_async_copy(amps_ref.at[span], held.at[span], load_sems.at[i])

    for i in range(chunks):
        load(i).start()

    barrier = pltpu.get_barrier_semaphore()

    def greet(step, carry):
        pl.semaphore_signal(barrier, inc=1, device_id=place(step), device_id_type=MESH)
        return carry

    lax.fori_loop(1, count, greet, 0)

    def block(i):
        span = pl.ds(pl.multiple_of(i * rows, rows), rows)
        return lax.dot_general(
            ints_ref[span], held[span], (((0,), (0,)), ((), ())), preferred_element_type=jnp.float32
        )

    load(0).wait()
    product[...] = block(0)

    pl.semaphore_wait(barrier, count - 1)

    def copy(step, slot):
        return pltpu.make_async_remote_copy(
            src_ref=own_ref,
            dst_ref=out_ref.at[slot],
            send_sem=send_sems.at[step],
            recv_sem=recv_sems.at[step],
            device_id=place(step),
            device_id_type=MESH,
        )

    def send(step, carry):
        copy(step, me).start()
        return carry

    lax.fori_loop(1, count, send, 0)
    out_ref[me] = own_ref[...]

    def accumulate(i, carry):
        load(i).wait()
        product[...] += block(i)
        return carry

    lax.fori_loop(1, chunks, accumulate, 0)

    def finish(step, carry):
        source = lax.rem(me + count - step, count)
        copy(step, source).wait_recv()
        copy(step, me).wait_send()
        return carry

    lax.fori_loop(1, count, finish, 0)

    per_device = own_ref.shape[0]
    total = jnp.zeros(own_ref.shape, jnp.float32)
    for d in range(count):
        total = total + out_ref[d].astype(jnp.float32) * product[d * per_device : (d + 1) * per_device]
    partial[...] = jnp.sum(total, axis=0, keepdims=True)

    def ecopy(step, slot):
        return pltpu.make_async_remote_copy(
            src_ref=partial,
            dst_ref=values.at[slot],
            send_sem=esend_sems.at[step],
            recv_sem=erecv_sems.at[step],
            device_id=place(step),
            device_id_type=MESH,
        )

    def esend(step, carry):
        ecopy(step, me).start()
        return carry

    lax.fori_loop(1, count, esend, 0)
    values[me] = partial[...]

    def efinish(step, carry):
        source = lax.rem(me + count - step, count)
        ecopy(step, source).wait_recv()
        ecopy(step, me).wait_send()
        return carry

    lax.fori_loop(1, count, efinish, 0)
    energy_ref[...] = jnp.sum(values[...], axis=0)


def gather(owned, integrals, amplitudes, nrows, ncols):
    count = nrows * ncols
    cells, pairs = amplitudes.shape
    window = integrals.shape[1]
    rows = largest_divisor(cells, ROWS, 8)
    size = amplitudes.dtype.itemsize
    limit = cells * pairs * size + 4 * window * pairs * 4 + 4 * MIB
    vmem = pl.BlockSpec(memory_space=pltpu.VMEM)
    dma = pltpu.SemaphoreType.DMA
    return pl.pallas_call(
        functools.partial(gather_kernel, nrows, ncols, rows),
        out_shape=(
            jax.ShapeDtypeStruct((count,) + owned.shape, owned.dtype),
            jax.ShapeDtypeStruct((1, pairs), jnp.float32),
        ),
        in_specs=[vmem, vmem, pl.BlockSpec(memory_space=pl.ANY)],
        out_specs=(vmem, vmem),
        scratch_shapes=[
            pltpu.VMEM((cells, pairs), amplitudes.dtype),
            pltpu.VMEM((window, pairs), jnp.float32),
            pltpu.VMEM((1, pairs), jnp.float32),
            pltpu.VMEM((count, 1, pairs), jnp.float32),
            dma((cells // rows,)),
            dma((count,)),
            dma((count,)),
            dma((count,)),
            dma((count,)),
        ],
        compiler_params=pltpu.CompilerParams(
            collective_id=0, has_side_effects=True, vmem_limit_bytes=limit
        ),
    )(owned, integrals, amplitudes)


def residual_kernel(ints_ref, cols_ref, out_ref):
    rows = out_ref.shape[0]
    start = pl.multiple_of(pl.program_id(0) * rows, 8)
    full = jnp.dot(ints_ref[pl.ds(start, rows)], cols_ref[...], preferred_element_type=jnp.float32)
    out_ref[...] = full.astype(out_ref.dtype)


def multiply(integrals, columns):
    cells, window = integrals.shape
    pairs = columns.shape[1]
    rows = largest_divisor(cells, OUT_ROWS, 8)
    vmem = pl.BlockSpec(memory_space=pltpu.VMEM)
    return pl.pallas_call(
        residual_kernel,
        grid=(cells // rows,),
        out_shape=jax.ShapeDtypeStruct((cells, pairs), jnp.bfloat16),
        in_specs=[vmem, vmem],
        out_specs=pl.BlockSpec((rows, pairs), lambda i: (i, 0)),
        compiler_params=pltpu.CompilerParams(
            dimension_semantics=("arbitrary",), vmem_limit_bytes=24 * MIB
        ),
    )(integrals, columns)


def shards(amplitudes, integrals, window_index):
    block_rows, block_cols, pairs = amplitudes.shape
    window = integrals.shape[2]
    ncols = lax.axis_size("col")
    nrows = lax.axis_size("row")
    per_device = window // (nrows * ncols)
    row_rank = lax.axis_index("row")
    col_rank = lax.axis_index("col")
    linear_rank = row_rank * ncols + col_rank
    owned_index = lax.dynamic_slice_in_dim(window_index, linear_rank * per_device, per_device)
    virtuals = block_rows * nrows
    row_offset = owned_index // virtuals - row_rank * block_rows
    col_offset = owned_index % virtuals - col_rank * block_cols
    owned = amplitudes[row_offset, col_offset]
    cells = block_rows * block_cols
    flat_ints = integrals.transpose(1, 0, 2).reshape(cells, window)
    columns, energy = gather(
        owned, flat_ints, amplitudes.transpose(1, 0, 2).reshape(cells, pairs), nrows, ncols
    )
    residual = multiply(flat_ints, columns.reshape(window, pairs))
    residual = residual.reshape(block_cols, block_rows, pairs).transpose(1, 0, 2)
    return (residual, energy[0] / virtuals)


def solution(mesh):
    return jax.shard_map(
        shards,
        mesh=mesh,
        in_specs=(P("row", "col", None), P("row", "col", None), P()),
        out_specs=(P("row", "col", None), P()),
        check_vma=False,
    )
```

time: 61.4 us -> 49.3 us (0.80)
  Pallas kernels: 56.1 us -> 41.8 us
  local copies, waits for them, and re-layouts: 1.97 us -> 5.27 us
  other arithmetic: 2.34 us -> 1.38 us
    pallas_call x3 -> x2, Pallas kernels: 56.1 us -> 41.8 us  [the longest x1 24.2 us: gather(): pl.pallas_call(functools.partial(gather_kernel, nrows, ncols, rows), out_...]
    unnamed x0 -> x2, local copies, waits for them, and re-layouts: none -> 3.9 us
    reduce_sum x1 -> x0, other arithmetic: 0.97 us -> none  [shards(): pair_energy = jnp.sum(values[:, 0, :], axis=0) / virtuals]
where the time goes in v1:
time: 49.3 us; the launch traced here: 49.1 us
  Pallas kernels  41.8 us (85%)
  local copies, waits for them, and re-layouts  5.27 us (11%)
  other arithmetic  1.38 us (3%)
  between operations  0.65 us (1%)
    pallas_call x1, Pallas kernels, gather(): pl.pallas_call(functools.partial(gather_kernel, nrows, ncols, rows), out_...  24.2 us
    pallas_call x1, Pallas kernels, multiply(): pl.pallas_call(residual_kernel, grid=(cells // rows,), out_shape=jax.Shap...  17.6 us
    unnamed x2, local copies, waits for them, and re-layouts  3.9 us
    gather x1, local copies, waits for them, and re-layouts, shards(): owned = amplitudes[row_offset, col_offset]  1.37 us

profile of v1, /device:TPU:0, one launch (start us, length us, event | category | flops | bytes accessed | tf_op | source)
XLA Modules:
  0.0 49.1 jit_solution(7265202780115887555)
XLA Ops:
  0.6 0.8 %fusion.3 = s32[8]{0:T(128)S(1)} fusion(s32[256]{0:T(256)} %param.5, s32[]{:T(128)S(6)} %select_n.21, s32[]{:T(128)S(6)} %mul.15, s32[]{:T(128)S(6)} %mul.14), kind=kLoop, calls=%fused_computation.9 | loop fusion | flops 200 | bytes 76 | tf_op jit(solution)/shard_map/concatenate | solution.py:196
  1.4 1.4 %gather_fusion = bf16[8,768]{1,0:T(8,128)(2,1)S(1)} fusion(bf16[200,100,768]{2,0,1:T(8,128)(2,1)} %param.3, s32[8]{0:T(128)S(1)} %fusion.3), kind=kCustom, calls=%fused_computation | custom fusion | bytes 24640 | tf_op jit(solution)/shard_map/gather | solution.py:196
  2.8 0.0 copy-start
  2.8 3.9 %copy-done = bf16[200,100,256]{2,0,1:T(8,128)(2,1)S(1)} copy-done((bf16[200,100,256]{2,0,1:T(8,128)(2,1)S(1)}, bf16[200,100,256]{2,0,1:T(8,128)(2,1)}, u32[]{:S(2)}) %copy-start) | copy-done | bytes 10240024
  6.7 24.2 %shard_map.50 = (bf16[32,8,768]{2,1,0:T(8,128)(2,1)S(1)}, f32[1,768]{1,0:T(1,128)S(1)}) custom-call(bf16[8,768]{1,0:T(8,128)(2,1)S(1)} %gather_fusion, bf16[20000,256]{1,0:T(8,128)(2,1)S(1)} %bitcast.10, bf16[20000,768]{1,0:T(8,128)(2,1)} %bitcast.13), custom_call_target="tpu_custom_call" | custom-call | tf_op jit(solution)/shard_map/pallas_call | solution.py:134
  30.9 17.6 %shard_map.51 = bf16[20000,768]{1,0:T(8,128)(2,1)} custom-call(bf16[20000,256]{1,0:T(8,128)(2,1)S(1)} %bitcast.11, bf16[256,768]{1,0:T(8,128)(2,1)S(1)} %bitcast.12), custom_call_target="tpu_custom_call" | custom-call | tf_op jit(solution)/shard_map/pallas_call | solution.py:171
  48.5 0.6 %multiply_reduce_fusion = f32[768]{0:T(1024)} fusion(f32[1,768]{1,0:T(1,128)S(1)} %get-tuple-element.5), kind=kLoop, calls=%fused_computation.1 | loop fusion | flops 768 | bytes 6144 | tf_op jit(solution)/shard_map/div | solution.py:204
Async XLA Ops:
  2.8 3.9 %copy-start = (bf16[200,100,256]{2,0,1:T(8,128)(2,1)S(1)}, bf16[200,100,256]{2,0,1:T(8,128)(2,1)}, u32[]{:S(2)}) copy-start(bf16[200,100,256]{2,0,1:T(8,128)(2,1)} %param.4) | copy-start | bytes 30720004
